TPU v7x, 32 devices: a whole 2x2x4 slice. The times are simulated.
32 devices in a mesh: dp: 4 (over x, core), mp: 8 (over z, y).
Axes of the slice: x: 2, y: 2, z: 4, core: 2. Of those that a mesh axis runs over, the one named last changes fastest.
Arguments:
- tokens: bfloat16 [1280, 1792], P(('dp', 'mp')), may hold values from -6 to 6
- norm_gain: float32 [1792], replicated, may hold values from 0.5 to 1.5
- norm_bias: float32 [1792], replicated, may hold values from -3 to 3
- w_in: bfloat16 [1792, 15360], P('dp', 'mp'), may hold values from -0.125 to 0.125
- b_in: float32 [15360], P('mp'), may hold values from -3 to 3
- w_out: bfloat16 [15360, 1792], P('mp', 'dp'), may hold values from -0.046875 to 0.046875
- b_out: float32 [1792], replicated, may hold values from -3 to 3
Outputs:
- result: bfloat16 [1280, 1792], P(('dp', 'mp'))
All inputs are finite; a program needn't handle non-finite values.
Results may differ from a plain program's by a relative error of at most 0.0042.
Values may be sent and summed in bfloat16 or wider, within the bound.
A program may use at most 128 MiB of HBM per device.

v0:
```python
import functools

import jax
import jax.numpy as jnp
from jax import lax
from jax.experimental import pallas as pl
from jax.experimental.pallas import tpu as pltpu
from jax.sharding import PartitionSpec as P

MESH = pl.DeviceIdType.MESH
LANES = 128
VMEM_GRANT = 60 * 2**20


def flip(index, mask, size):
    out, bit = index, 1
    while bit < size:
        if mask & bit:
            out = out + bit - 2 * bit * (lax.rem(lax.div(index, bit), 2))
        bit *= 2
    return out


def gelu(pre):
    return 0.5 * pre * (1.0 + lax.erf(pre * (0.5**0.5)))


def kernel(
    lines, tokens, gain, bias, w_in, b_in, w_out, b_out, out,
    shift, tok, win, wout, normed, hidden, part, own, from_y, sums, from_z, to_x, kept, from_x,
    tok_sem, win_sem, wout_sem, y_sem, z_sem, x_sem, local_sem, send_sem,
):
    dp, mp = lax.axis_index("dp"), lax.axis_index("mp")
    x, core = lax.div(dp, 2), lax.rem(dp, 2)
    z, y = lax.div(mp, 2), lax.rem(mp, 2)
    ox, oy = 1 - x, 1 - y
    rows, depth = tokens.shape[0], w_in.shape[0]
    units = w_in.shape[1]
    half = units // 2
    start = half // LANES * LANES
    width = units - start
    x_dev = (2 * ox + core, mp)
    core_dev = (2 * x + 1 - core, mp)
    y_dev = (dp, 2 * z + oy)
    z_at = [flip(z, k, lines) for k in range(lines)]
    z_dev = [(dp, 2 * z_at[k] + y) for k in range(lines)]

    barrier = pltpu.get_barrier_semaphore()
    partners = [x_dev, core_dev, y_dev] + z_dev[1:]
    for partner in partners:
        pl.semaphore_signal(barrier, inc=1, device_id=partner, device_id_type=MESH)
    pl.semaphore_wait(barrier, len(partners))

    sends = []

    def send(src, dst, sem, device):
        copy = pltpu.make_async_remote_copy(
            src_ref=src, dst_ref=dst, send_sem=send_sem.at[len(sends)], recv_sem=sem,
            device_id=device, device_id_type=MESH,
        )
        copy.start()
        sends.append(copy)

    def arrive(dst, sem):
        pltpu.make_async_remote_copy(
            src_ref=dst, dst_ref=dst, send_sem=send_sem.at[0], recv_sem=sem,
            device_id=x_dev, device_id_type=MESH,
        ).wait_recv()

    def slot(yy, zz, side):
        return (yy * lines + zz) * 2 + side

    mine = tok.at[slot(y, z, x)]
    mine_sem = tok_sem.at[y, z, x]
    send(tokens, mine, mine_sem, x_dev)
    for k in range(1, lines):
        send(tokens, mine, mine_sem, z_dev[k])
    send(tokens, mine, mine_sem, y_dev)
    locals_ = [pltpu.make_async_copy(tokens, mine, local_sem.at[0])]

    def columns(weight, side):
        return weight.at[:, pl.ds(pl.multiple_of(side * start, LANES), width)]


    def rows_of(full, owner):
        return full.at[pl.ds(pl.multiple_of(owner * depth, 16), depth), :]

    far, near, across = 2 * ox + core, 2 * x + 1 - core, 2 * ox + 1 - core
    send(columns(w_in, ox), rows_of(win, dp), win_sem.at[dp], x_dev)
    send(columns(w_in, x), rows_of(win, dp), win_sem.at[dp], core_dev)
    send(columns(w_out, ox), rows_of(wout, dp), wout_sem.at[dp], x_dev)
    send(columns(w_out, x), rows_of(wout, dp), wout_sem.at[dp], core_dev)
    locals_.append(pltpu.make_async_copy(columns(w_in, x), rows_of(win, dp), local_sem.at[1]))
    locals_.append(pltpu.make_async_copy(columns(w_out, x), rows_of(wout, dp), local_sem.at[2]))
    for copy in locals_:
        copy.start()

    shift[...] = jnp.broadcast_to(b_in[...], shift.shape)

    arrive(tok.at[slot(y, z, ox)], tok_sem.at[y, z, ox])
    for k in range(1, lines):
        send(tok.at[slot(y, z, ox)], tok.at[slot(y, z, ox)], tok_sem.at[y, z, ox], z_dev[k])
    send(tok.at[slot(y, z, ox)], tok.at[slot(y, z, ox)], tok_sem.at[y, z, ox], y_dev)
    for side in (x, ox):
        for k in range(1, lines):
            block, sem = tok.at[slot(y, z_at[k], side)], tok_sem.at[y, z_at[k], side]
            arrive(block, sem)
            send(block, block, sem, y_dev)

    def normalise(yy, zz):
        pair = jnp.concatenate(
            [tok[slot(yy, zz, 0)].astype(jnp.float32), tok[slot(yy, zz, 1)].astype(jnp.float32)], axis=0
        )
        center = jnp.mean(pair, axis=1, keepdims=True)
        spread = jnp.mean((pair - center) ** 2, axis=1, keepdims=True)
        value = (pair - center) / jnp.sqrt(spread + 1e-06) * gain[...] + bias[...]
        normed[yy, pl.ds(pl.multiple_of(zz * 2 * rows, 16), 2 * rows), :] = value.astype(
            normed.dtype
        )

    tile = 2 * LANES if width % (2 * LANES) == 0 else LANES

    def first(yy):
        def step(n, carry):
            at = pl.ds(pl.multiple_of(n * tile, LANES), tile)
            pre = jnp.dot(normed[yy], win[:, at], preferred_element_type=jnp.float32)
            pre = pre + shift[:1, pl.ds(pl.multiple_of(x * start + n * tile, LANES), tile)]
            unit = x * start + n * tile + lax.broadcasted_iota(jnp.int32, pre.shape, 1)
            keep = (unit >= x * half) & (unit < (x + 1) * half)
            hidden[yy, :, at] = jnp.where(keep, gelu(pre), 0.0).astype(hidden.dtype)
            return carry

        lax.fori_loop(0, width // tile, step, 0)

    locals_[0].wait()

    def norm_own(zz, carry):
        normalise(y, zz)
        return carry

    lax.fori_loop(0, lines, norm_own, 0)

    arrive(rows_of(win, far), win_sem.at[far])
    send(rows_of(win, far), rows_of(win, far), win_sem.at[far], core_dev)
    locals_[1].wait()
    arrive(rows_of(win, near), win_sem.at[near])
    arrive(rows_of(win, across), win_sem.at[across])
    first(y)

    for k in range(lines):
        for side in (x, ox):
            arrive(tok.at[slot(oy, z_at[k], side)], tok_sem.at[oy, z_at[k], side])
        normalise(oy, z_at[k])
    first(oy)

    def second(q, yy, zz):
        side = x if q == 0 else ox
        act = hidden[yy, pl.ds(pl.multiple_of(zz * 2 * rows, 16), 2 * rows), :]
        weight = wout[pl.ds(pl.multiple_of(side * 2 * depth, 16), 2 * depth), :]
        return lax.dot_general(
            act, weight, (((1,), (1,)), ((), ())), preferred_element_type=jnp.float32
        )

    def product(q):
        for k in range(lines):
            part[q, z_at[k]] = second(q, oy, z_at[k]).astype(part.dtype)
            send(part.at[q, z_at[k]], from_y.at[q, z_at[k]], y_sem.at[q, z_at[k]], y_dev)

        def step(zz, carry):
            own[q, zz] = second(q, y, zz)
            return carry

        lax.fori_loop(0, lines, step, 0)

    def along_z(q):
        for k in list(range(1, lines)) + [0]:
            at = z_at[k]
            arrive(from_y.at[q, at], y_sem.at[q, at])
            total = own[q, at] + from_y[q, at].astype(jnp.float32)
            if k:
                sums[q, at] = total.astype(sums.dtype)
                send(sums.at[q, at], from_z.at[q, z], z_sem.at[q, z], z_dev[k])
            else:
                own[q, at] = total

    def along_x(q):
        side = x if q == 0 else ox
        total = own[q, z]
        for k in range(1, lines):
            arrive(from_z.at[q, z_at[k]], z_sem.at[q, z_at[k]])
            total = total + from_z[q, z_at[k]].astype(jnp.float32)
        own[q, z] = total
        to_x[q] = own[q, z, pl.ds(pl.multiple_of(ox * rows, 8), rows), :].astype(to_x.dtype)
        send(to_x.at[q], from_x.at[side], x_sem.at[side], x_dev)
        kept[side] = own[q, z, pl.ds(pl.multiple_of(x * rows, 8), rows), :]

    locals_[2].wait()
    arrive(rows_of(wout, near), wout_sem.at[near])
    product(0)
    arrive(rows_of(wout, far), wout_sem.at[far])
    send(rows_of(wout, far), rows_of(wout, far), wout_sem.at[far], core_dev)
    along_z(0)
    arrive(rows_of(wout, across), wout_sem.at[across])
    product(1)
    along_x(0)
    along_z(1)
    along_x(1)
    columns_of, added = 2 * depth, b_out[...]
    for side in range(2):
        at = slice(side * columns_of, (side + 1) * columns_of)
        arrive(from_x.at[side], x_sem.at[side])
        total = kept[side] + from_x[side].astype(jnp.float32)
        out[:, at] = tok[slot(y, z, x), :, at].astype(jnp.float32) + total + added[:, at]
    for copy in sends:
        copy.wait_send()


def fused(mp, tokens, gain, bias, w_in, b_in, w_out, b_out):
    rows, dim = tokens.shape
    depth, units = w_in.shape
    lines = mp // 2
    width = units - units // 2 // LANES * LANES
    columns = 2 * depth
    bf16, f32, dma = jnp.bfloat16, jnp.float32, pltpu.SemaphoreType.DMA
    vmem = pl.BlockSpec(memory_space=pltpu.VMEM)
    hbm = pl.BlockSpec(memory_space=pl.ANY)
    n_sends = (lines + 1) * 2 + 4 + 2 * (lines - 1) + 2 + 2 * (lines + lines - 1 + 1)
    return pl.pallas_call(
        functools.partial(kernel, lines),
        out_shape=jax.ShapeDtypeStruct((rows, dim), f32),
        in_specs=[hbm, vmem, vmem, hbm, vmem, hbm, vmem],
        out_specs=vmem,
        scratch_shapes=[
            pltpu.VMEM((8, units), f32),
            pltpu.VMEM((4 * lines + 1, rows, dim), bf16),
            pltpu.VMEM((dim, width), bf16),
            pltpu.VMEM((dim, width), bf16),
            pltpu.VMEM((2, lines * 2 * rows, dim), bf16),
            pltpu.VMEM((2, lines * 2 * rows, width), bf16),
            pltpu.VMEM((2, lines, 2 * rows, columns), bf16),
            pltpu.VMEM((2, lines, 2 * rows, columns), f32),
            pltpu.VMEM((2, lines, 2 * rows, columns), bf16),
            pltpu.VMEM((2, lines, 2 * rows, columns), bf16),
            pltpu.VMEM((2, lines, 2 * rows, columns), bf16),
            pltpu.VMEM((3, rows, columns), bf16),
            pltpu.VMEM((2, rows, columns), f32),
            pltpu.VMEM((3, rows, columns), bf16),
            dma((2, lines, 2)),
            dma((4,)),
            dma((4,)),
            dma((2, lines)),
            dma((2, lines)),
            dma((2,)),
            dma((3,)),
            dma((n_sends,)),
        ],
        compiler_params=pltpu.CompilerParams(
            collective_id=0, has_side_effects=True, vmem_limit_bytes=VMEM_GRANT
        ),
    )(tokens, gain[None], bias[None], w_in, b_in[None], w_out.T, b_out[None]).astype(bf16)


def gathered(tokens, norm_gain, norm_bias, w_in, b_in, w_out, b_out):
    values = tokens.astype(jnp.float32)
    center = jnp.mean(values, axis=1, keepdims=True)
    spread = jnp.mean((values - center) ** 2, axis=1, keepdims=True)
    normed = ((values - center) / jnp.sqrt(spread + 1e-06) * norm_gain + norm_bias).astype(
        jnp.bfloat16
    )
    w_in_full = lax.all_gather(w_in, "dp", axis=0, tiled=True)
    everyone = lax.all_gather(normed, "mp", axis=0, tiled=True)
    pre = jnp.dot(everyone, w_in_full, preferred_element_type=jnp.float32) + b_in
    hidden = jax.nn.gelu(pre, approximate=False).astype(jnp.bfloat16)
    w_out_full = lax.all_gather(w_out, "dp", axis=1, tiled=True)
    summed = lax.psum_scatter(
        jnp.dot(hidden, w_out_full, preferred_element_type=jnp.float32),
        "mp",
        scatter_dimension=0,
        tiled=True,
    )
    return (values + summed + b_out).astype(jnp.bfloat16)


def on_device(dp, mp, tokens, norm_gain, norm_bias, w_in, b_in, w_out, b_out):
    rows, (depth, units) = tokens.shape[0], w_in.shape
    fits = (
        dp == 4
        and mp % 2 == 0
        and mp & (mp - 1) == 0
        and units % LANES == 0
        and depth % 16 == 0
        and 2 * depth % LANES == 0
        and rows % 8 == 0
        and mp * 2 * rows * (2 * depth) * 2 * 24 < VMEM_GRANT
    )
    if fits:
        return fused(mp, tokens, norm_gain, norm_bias, w_in, b_in, w_out, b_out)
    return gathered(tokens, norm_gain, norm_bias, w_in, b_in, w_out, b_out)


def solution(mesh):
    placed = (P(("dp", "mp"), None), P(), P(), P("dp", "mp"), P("mp"), P("mp", "dp"), P())
    return jax.shard_map(
        functools.partial(on_device, mesh.shape["dp"], mesh.shape["mp"]),
        mesh=mesh,
        in_specs=placed,
        out_specs=P(("dp", "mp"), None),
        check_vma=False,
    )
```

profile of v0, /device:TPU:0, one launch (start us, length us, event | category | flops | bytes accessed | tf_op | source)
XLA Modules:
  0.0 90.9 jit_solution(13100046481779803007)
XLA Ops:
  0.0 1.3 %broadcast_in_dim.12.gain = f32[1,1792]{1,0:T(1,128)} reshape(f32[1792]{0:T(1024)} %param.8) | data formatting | bytes 14336 | tf_op jit(solution)/shard_map/broadcast_in_dim | solution.py:260
  1.3 1.3 %broadcast_in_dim.13.bias = f32[1,1792]{1,0:T(1,128)} reshape(f32[1792]{0:T(1024)} %param.9) | data formatting | bytes 14336 | tf_op jit(solution)/shard_map/broadcast_in_dim | solution.py:260
  2.6 1.3 %broadcast_in_dim.15.b_out = f32[1,1792]{1,0:T(1,128)} reshape(f32[1792]{0:T(1024)} %param.13) | data formatting | bytes 14336 | tf_op jit(solution)/shard_map/broadcast_in_dim | solution.py:260
  3.9 1.3 %broadcast_in_dim.14.b_in = f32[1,1920]{1,0:T(1,128)} reshape(f32[1920]{0:T(1024)} %param.11) | data formatting | bytes 15360 | tf_op jit(solution)/shard_map/broadcast_in_dim | solution.py:260
  5.2 84.1 %shard_map.73 = f32[40,1792]{1,0:T(8,128)} custom-call(bf16[40,1792]{1,0:T(8,128)(2,1)} %tokens.1, f32[1,1792]{1,0:T(1,128)} %broadcast_in_dim.12.gain, f32[1,1792]{1,0:T(1,128)} %broadcast_in_dim.13.bias, bf16[448,1920]{1,0:T(8,128)(2,1)} %w_in.1, f32[1,1920]{1,0:T(1,128)} %broadcast_in_dim.14.b_in, bf16[448,1920]{1,0:T(8,128)(2,1)} %bitcast.1, ...), custom_call_target="tpu_custom_call" | custom-call | tf_op jit(solution)/shard_map/pallas_call | solution.py:228
  89.3 1.6 %convert_element_type.3 = bf16[40,1792]{1,0:T(8,128)(2,1)} convert(f32[40,1792]{1,0:T(8,128)} %shard_map.73) | non-fusion elementwise | flops 71680 | bytes 430080 | tf_op jit(solution)/shard_map/convert_element_type | solution.py:260
where the time goes:
time: 91.4 us; the launch traced here: 90.9 us
  Pallas kernels  84.1 us (92%)
  local copies, waits for them, and re-layouts  5.18 us (6%)
  other arithmetic  1.63 us (2%)
    pallas_call x1, Pallas kernels, fused(): pl.pallas_call(functools.partial(kernel, lines), out_shape=jax.ShapeDtype...  84.1 us

commit v1 on v0

v1 whole, which is shorter than its diff:
```python
import functools

import jax
import jax.numpy as jnp
from jax import lax
from jax.experimental import pallas as pl
from jax.experimental.pallas import tpu as pltpu
from jax.sharding import PartitionSpec as P

MESH = pl.DeviceIdType.MESH
LANES = 128
VMEM_GRANT = 60 * 2**20


def flip(index, mask, size):
    out, bit = index, 1
    while bit < size:
        if mask & bit:
            out = out + bit - 2 * bit * (lax.rem(lax.div(index, bit), 2))
        bit *= 2
    return out


def column_chunks(depth):
    full, rest = depth // LANES, depth % LANES
    if rest:
        return [(t, t + full + 1) for t in range(full)] + [(full,)]
    return [(t, t + full) for t in range(full)]


def gelu(pre):
    return 0.5 * pre * (1.0 + lax.erf(pre * (0.5**0.5)))


def kernel(
    lines, tokens, gain, bias, w_in, b_in, w_out, b_out, out,
    vec, tok, win, wout, normed, hidden, part, own, from_y, sums, from_z, to_x, kept, from_x,
    tok_sem, win_sem, wout_sem, near_sem, y_sem, z_sem, x_sem, local_sem, send_sem,
):
    dp, mp = lax.axis_index("dp"), lax.axis_index("mp")
    x, core = lax.div(dp, 2), lax.rem(dp, 2)
    z, y = lax.div(mp, 2), lax.rem(mp, 2)
    ox, oy = 1 - x, 1 - y
    rows, dim = tokens.shape
    depth, units = w_in.shape
    half = units // 2
    start = half // LANES * LANES
    width = units - start
    tile = 2 * LANES if width % (2 * LANES) == 0 else LANES
    tiles = width // tile
    last = lines - 1
    side_columns = 2 * depth
    chunks = column_chunks(depth)
    per_side = len(chunks)
    full, rest = depth // LANES, depth % LANES
    pair_rows = 2 * rows

    x_dev = (2 * ox + core, mp)
    core_dev = (2 * x + 1 - core, mp)
    y_dev = (dp, 2 * z + oy)
    up_dev, down_dev = (dp, 2 * (z + 1) + y), (dp, 2 * (z - 1) + y)
    z_at = [flip(z, k, lines) for k in range(lines)]
    z_dev = [(dp, 2 * z_at[k] + y) for k in range(lines)]
    has_up, has_down = z < last, z > 0

    sends = []

    def send(src, dst, sem, device, when=None):
        copy = pltpu.make_async_remote_copy(
            src_ref=src, dst_ref=dst, send_sem=send_sem.at[len(sends)], recv_sem=sem,
            device_id=device, device_id_type=MESH,
        )
        sends.append((copy, when))
        if when is None:
            copy.start()
        else:
            pl.when(when)(copy.start)

    def arrive(dst, sem):
        pltpu.make_async_remote_copy(
            src_ref=dst, dst_ref=dst, send_sem=send_sem.at[0], recv_sem=sem,
            device_id=x_dev, device_id_type=MESH,
        ).wait_recv()

    def local(src, dst, at):
        copy = pltpu.make_async_copy(src, dst, local_sem.at[at])
        copy.start()
        return copy

    def block(r, zz, side):
        return tok.at[r, zz, side], tok_sem.at[r, zz, side]

    def own_columns(weight):
        return weight.at[:, pl.ds(pl.multiple_of(x * start, LANES), width)]

    def rows_of(weight, owner):
        return weight.at[pl.ds(pl.multiple_of(owner * depth, 16), depth), :]

    def in_tile(weight, owner, n):
        return weight.at[pl.ds(pl.multiple_of(owner * depth, 16), depth), pl.ds(n * tile, tile)]

    def out_rows(owner_core, m):
        if rest and m == full:
            return pl.multiple_of((1 - owner_core) * full * LANES, 16), rest
        return pl.multiple_of(owner_core * rest + m * LANES, 16), LANES

    def out_chunk(weight, owner, owner_core, m):
        at, size = out_rows(owner_core, m)
        return weight.at[pl.ds(pl.multiple_of(owner * depth + at, 16), size), :]

    small = [
        local(ref, vec.at[i, pl.ds(0, ref.shape[0])], i)
        for i, ref in enumerate((gain, bias, b_in, b_out))
    ]
    copies = [
        local(tokens, tok.at[0, z, 0], 4),
        local(own_columns(w_in), rows_of(win, dp), 5),
        local(own_columns(w_out), rows_of(wout, dp), 6),
    ]

    barrier = pltpu.get_barrier_semaphore()
    for partner in (x_dev, core_dev, y_dev):
        pl.semaphore_signal(barrier, inc=1, device_id=partner, device_id_type=MESH)
    for partner, exists in ((up_dev, has_up), (down_dev, has_down)):
        pl.when(exists)(
            functools.partial(
                pl.semaphore_signal, barrier, inc=1, device_id=partner, device_id_type=MESH
            )
        )
    pl.semaphore_wait(barrier, 3 + has_up.astype(jnp.int32) + has_down.astype(jnp.int32))

    copies[0].wait()
    mine = tok.at[0, z, 0]
    send(mine, tok.at[0, z, 1], tok_sem.at[0, z, 1], x_dev)
    send(mine, mine, tok_sem.at[0, z, 0], up_dev, has_up)
    send(mine, mine, tok_sem.at[0, z, 0], down_dev, has_down)
    send(mine, tok.at[1, z, 0], tok_sem.at[1, z, 0], y_dev)
    far, near, across = 2 * ox + core, 2 * x + 1 - core, 2 * ox + 1 - core
    for n in range(tiles):
        at = pl.ds(pl.multiple_of(ox * start + n * tile, LANES), tile)
        send(w_in.at[:, at], in_tile(win, dp, n), win_sem.at[n, dp], x_dev)
    for m in range(per_side):
        at, size = out_rows(core, m)
        columns = pl.ds(pl.multiple_of(ox * start, LANES), width)
        send(w_out.at[pl.ds(at, size), columns], out_chunk(wout, dp, core, m), wout_sem.at[m, dp], x_dev)
    send(own_columns(w_in), rows_of(win, dp), near_sem.at[0], core_dev)
    send(own_columns(w_out), rows_of(wout, dp), near_sem.at[1], core_dev)

    def forward(zz, side, up, exists=None):
        def go():
            arrive(*block(0, zz, side))

        if exists is None:
            go()
        else:
            pl.when(exists)(go)
        ref, sem = block(0, zz, side)
        further = has_up if up else has_down
        along = further if exists is None else jnp.logical_and(exists, further)
        send(ref, ref, sem, up_dev if up else down_dev, along)
        ends = 0 if up else last
        cross = exists
        if side:
            cross = jnp.logical_and(exists, zz != ends)
        send(ref, tok.at[1, zz, side], tok_sem.at[1, zz, side], y_dev, cross)

    def from_line(d, side):
        forward(z - d, side, True, z >= d)
        forward(z + d, side, False, z + d <= last)

    def normalise(r, k):
        pair = jnp.concatenate(
            [tok[r, z_at[k], 0].astype(jnp.float32), tok[r, z_at[k], 1].astype(jnp.float32)], axis=0
        )
        center = jnp.mean(pair, axis=1, keepdims=True)
        spread = jnp.mean((pair - center) ** 2, axis=1, keepdims=True)
        value = (pair - center) / jnp.sqrt(spread + 1e-06) * vec[0:1, :dim] + vec[1:2, :dim]
        normed[r, pl.ds(k * pair_rows, pair_rows), :] = value.astype(normed.dtype)

    def arrive_over_y(k):
        zz = z_at[k]
        arrive(*block(1, zz, 0))
        arrive(*block(1, zz, 1))
        ref, sem = block(1, zz, 1)
        send(ref, ref, sem, up_dev, jnp.logical_and(zz == 0, has_up))
        send(ref, ref, sem, down_dev, jnp.logical_and(zz == last, has_down))

    def activate(lhs, n):
        at = pl.ds(n * tile, tile)
        pre = jnp.dot(lhs, win[:, at], preferred_element_type=jnp.float32)
        first = pl.multiple_of(x * start + n * tile, LANES)
        pre = pre + vec[2:3, pl.ds(first, tile)]
        unit = first + lax.broadcasted_iota(jnp.int32, pre.shape, 1)
        keep = (unit >= x * half) & (unit < (x + 1) * half)
        return jnp.where(keep, gelu(pre), 0.0).astype(hidden.dtype)

    def first_pair(k, n):
        at = pl.ds(k * pair_rows, pair_rows)
        value = activate(jnp.concatenate([normed[0, at, :], normed[1, at, :]], axis=0), n)
        hidden[0, at, pl.ds(n * tile, tile)] = value[:pair_rows]
        hidden[1, at, pl.ds(n * tile, tile)] = value[pair_rows:]

    def first_all(n):
        everyone = normed[...].reshape(2 * lines * pair_rows, dim)
        value = activate(everyone, n)
        hidden[:, :, pl.ds(n * tile, tile)] = value.reshape(2, lines * pair_rows, tile)

    def tile_forward(n):
        arrive(in_tile(win, far, n), win_sem.at[n, far])
        send(in_tile(win, far, n), in_tile(win, far, n), win_sem.at[n, far], core_dev)

    def tile_ready(n):
        arrive(in_tile(win, across, n), win_sem.at[n, across])

    def weights(side, m):
        return jnp.concatenate(
            [
                wout[pl.ds(pl.multiple_of(side * side_columns + t * LANES, LANES), LANES), :]
                for t in chunks[m]
            ],
            axis=0,
        )

    def cols(m):
        return pl.ds(0, len(chunks[m]) * LANES)

    def product(q, m):
        j = q * per_side + m
        weight = weights(x if q == 0 else ox, m)

        def second(r):
            value = lax.dot_general(
                hidden[r], weight, (((1,), (1,)), ((), ())), preferred_element_type=jnp.float32
            )
            return value.reshape(lines, pair_rows, -1)

        part[j, :, :, cols(m)] = second(1).astype(part.dtype)
        send(part.at[j, :, :, cols(m)], from_y.at[j, :, :, cols(m)], y_sem.at[j], y_dev)
        own[j, :, :, cols(m)] = second(0)

    def along_z(q, m):
        j, c = q * per_side + m, cols(m)
        arrive(from_y.at[j, :, :, c], y_sem.at[j])
        for k in list(range(lines - 1, 0, -1)) + [0]:
            total = own[j, k, :, c] + from_y[j, k, :, c].astype(jnp.float32)
            if k:
                sums[j, k, :, c] = total.astype(sums.dtype)
                send(sums.at[j, k, :, c], from_z.at[j, k, :, c], z_sem.at[j, k], z_dev[k])
            else:
                own[j, 0, :, c] = total

    def along_x(q, m):
        j, c = q * per_side + m, cols(m)
        theirs = (1 - q) * per_side + m
        total = own[j, 0, :, c]
        for k in range(1, lines):
            arrive(from_z.at[j, k, :, c], z_sem.at[j, k])
            total = total + from_z[j, k, :, c].astype(jnp.float32)
        kept[j, :, c] = total[:rows]
        to_x[j, :, c] = total[rows:].astype(to_x.dtype)
        send(to_x.at[j, :, c], from_x.at[theirs, :, c], x_sem.at[theirs], x_dev)

    def finish(q, m):
        j, c = q * per_side + m, cols(m)
        side = x if q == 0 else ox
        arrive(from_x.at[j, :, c], x_sem.at[j])
        total = kept[j, :, c] + from_x[j, :, c].astype(jnp.float32)
        for i, t in enumerate(chunks[m]):
            at = pl.ds(pl.multiple_of(side * side_columns + t * LANES, LANES), LANES)
            value = tok[0, z, 0, :, at].astype(jnp.float32) + total[:, i * LANES:(i + 1) * LANES]
            out[:, at] = (value + vec[3:4, at]).astype(out.dtype)

    def own_block():
        ref, sem = block(0, z, 1)
        arrive(ref, sem)
        send(ref, ref, sem, up_dev, has_up)
        send(ref, ref, sem, down_dev, has_down)
        send(ref, tok.at[1, z, 1], tok_sem.at[1, z, 1], y_dev)

    def out_forward(m):
        arrive(out_chunk(wout, far, core, m), wout_sem.at[m, far])
        send(out_chunk(wout, far, core, m), out_chunk(wout, far, core, m), wout_sem.at[m, far], core_dev)

    def out_ready(m):
        arrive(out_chunk(wout, across, 1 - core, m), wout_sem.at[m, across])

    own_block()
    from_line(1, 0)
    for copy in small:
        copy.wait()
    normalise(0, 0)
    from_line(1, 1)
    arrive_over_y(0)
    done, known, ready = set(), [0], 0

    def catch_up():
        for k in known:
            for n in range(ready):
                if (k, n) not in done:
                    first_pair(k, n)
                    done.add((k, n))

    for d in range(1, lines):
        n = d - 1
        if n < tiles - 1:
            tile_forward(n)
        if d == 1:
            normalise(1, 0)
            copies[1].wait()
            arrive(rows_of(win, near), near_sem.at[0])
        if d + 1 < lines:
            from_line(d + 1, 0)
        if n < tiles - 1:
            tile_ready(n)
            ready = n + 1
        normalise(0, d)
        catch_up()
        if d + 1 < lines:
            from_line(d + 1, 1)
        if d < last:
            arrive_over_y(d)
            normalise(1, d)
            known.append(d)
    for n in range(ready, tiles - 1):
        tile_forward(n)
        tile_ready(n)
    ready = tiles - 1
    catch_up()
    tile_forward(tiles - 1)
    arrive_over_y(last)
    normalise(1, last)
    known.append(last)
    catch_up()
    tile_ready(tiles - 1)
    first_all(tiles - 1)

    copies[2].wait()
    arrive(rows_of(wout, near), near_sem.at[1])
    order = [(q, m) for q in range(2) for m in range(per_side)]
    n = len(order)
    for m in range(per_side):
        product(0, m)
    summed = crossed = 0
    for m in range(per_side):
        out_forward(m)
        along_z(*order[summed])
        summed += 1
        if m > 1:
            along_x(*order[crossed])
            crossed += 1
        out_ready(m)
        product(1, m)
    while crossed < n:
        if summed < n:
            along_z(*order[summed])
            summed += 1
        along_x(*order[crossed])
        crossed += 1
    for q, m in [(q, m) for m in range(per_side) for q in range(2)]:
        finish(q, m)
    for copy, when in sends:
        if when is None:
            copy.wait_send()
        else:
            pl.when(when)(copy.wait_send)


def fused(mp, tokens, gain, bias, w_in, b_in, w_out, b_out):
    rows, dim = tokens.shape
    depth, units = w_in.shape
    lines = mp // 2
    width = units - units // 2 // LANES * LANES
    chunks = column_chunks(depth)
    n, cols = 2 * len(chunks), max(len(c) for c in chunks) * LANES
    tiles = width // LANES
    bf16, f32, dma = jnp.bfloat16, jnp.float32, pltpu.SemaphoreType.DMA
    hbm = pl.BlockSpec(memory_space=pl.ANY)
    n_sends = 16 + 8 * lines + 2 * tiles + 2 * n + n * (lines + 1)
    return pl.pallas_call(
        functools.partial(kernel, lines),
        out_shape=jax.ShapeDtypeStruct((rows, dim), bf16),
        in_specs=[hbm] * 7,
        out_specs=pl.BlockSpec(memory_space=pltpu.VMEM),
        scratch_shapes=[
            pltpu.VMEM((4, max(dim, units)), f32),
            pltpu.VMEM((2, lines, 2, rows, dim), bf16),
            pltpu.VMEM((dim, width), bf16),
            pltpu.VMEM((dim, width), bf16),
            pltpu.VMEM((2, lines * 2 * rows, dim), bf16),
            pltpu.VMEM((2, lines * 2 * rows, width), bf16),
            pltpu.VMEM((n, lines, 2 * rows, cols), bf16),
            pltpu.VMEM((n, lines, 2 * rows, cols), f32),
            pltpu.VMEM((n, lines, 2 * rows, cols), bf16),
            pltpu.VMEM((n, lines, 2 * rows, cols), bf16),
            pltpu.VMEM((n, lines, 2 * rows, cols), bf16),
            pltpu.VMEM((n, rows, cols), bf16),
            pltpu.VMEM((n, rows, cols), f32),
            pltpu.VMEM((n, rows, cols), bf16),
            dma((2, lines, 2)),
            dma((tiles, 4)),
            dma((len(chunks), 4)),
            dma((2,)),
            dma((n,)),
            dma((n, lines)),
            dma((n,)),
            dma((7,)),
            dma((n_sends,)),
        ],
        compiler_params=pltpu.CompilerParams(
            collective_id=0, has_side_effects=True, vmem_limit_bytes=VMEM_GRANT
        ),
    )(tokens, gain, bias, w_in, b_in, w_out.T, b_out)


def gathered(tokens, norm_gain, norm_bias, w_in, b_in, w_out, b_out):
    values = tokens.astype(jnp.float32)
    center = jnp.mean(values, axis=1, keepdims=True)
    spread = jnp.mean((values - center) ** 2, axis=1, keepdims=True)
    normed = ((values - center) / jnp.sqrt(spread + 1e-06) * norm_gain + norm_bias).astype(
        jnp.bfloat16
    )
    w_in_full = lax.all_gather(w_in, "dp", axis=0, tiled=True)
    everyone = lax.all_gather(normed, "mp", axis=0, tiled=True)
    pre = jnp.dot(everyone, w_in_full, preferred_element_type=jnp.float32) + b_in
    hidden = jax.nn.gelu(pre, approximate=False).astype(jnp.bfloat16)
    w_out_full = lax.all_gather(w_out, "dp", axis=1, tiled=True)
    summed = lax.psum_scatter(
        jnp.dot(hidden, w_out_full, preferred_element_type=jnp.float32),
        "mp",
        scatter_dimension=0,
        tiled=True,
    )
    return (values + summed + b_out).astype(jnp.bfloat16)


def on_device(dp, mp, tokens, norm_gain, norm_bias, w_in, b_in, w_out, b_out):
    rows, (depth, units) = tokens.shape[0], w_in.shape
    fits = (
        dp == 4
        and mp % 2 == 0
        and mp & (mp - 1) == 0
        and units % LANES == 0
        and depth % 16 == 0
        and 2 * depth % LANES == 0
        and 2 * (depth % LANES) in (0, LANES)
        and mp >= 4
        and rows % 8 == 0
        and mp * 2 * rows * (2 * depth) * 2 * 24 < VMEM_GRANT
    )
    if fits:
        return fused(mp, tokens, norm_gain, norm_bias, w_in, b_in, w_out, b_out)
    return gathered(tokens, norm_gain, norm_bias, w_in, b_in, w_out, b_out)


def solution(mesh):
    placed = (P(("dp", "mp"), None), P(), P(), P("dp", "mp"), P("mp"), P("mp", "dp"), P())
    return jax.shard_map(
        functools.partial(on_device, mesh.shape["dp"], mesh.shape["mp"]),
        mesh=mesh,
        in_specs=placed,
        out_specs=P(("dp", "mp"), None),
        check_vma=False,
    )
```

time: 91.4 us -> 72.9 us (0.80)
  Pallas kernels: 84.1 us -> 71.2 us
  local copies, waits for them, and re-layouts: 5.18 us -> 1.58 us
  other arithmetic: 1.63 us -> 0 us
    pallas_call x1, Pallas kernels: 84.1 us -> 71.2 us  [fused(): pl.pallas_call(functools.partial(kernel, lines), out_shape=jax.ShapeDtype...]
    broadcast_in_dim x4 -> x0, local copies, waits for them, and re-layouts: 5.18 us -> none  [the longest x1 1.3 us: fused(): gain[None]]
    convert_element_type x1 -> x0, other arithmetic: 1.63 us -> none  [fused(): return pl.pallas_call(functools.partial(kernel, lines), out_shape=jax.Sha...]
    unnamed x0 -> x1, local copies, waits for them, and re-layouts: none -> 1.58 us
where the time goes in v1:
time: 72.9 us; the launch traced here: 72.8 us
  Pallas kernels  71.2 us (98%)
  local copies, waits for them, and re-layouts  1.58 us (2%)
    pallas_call x1, Pallas kernels, fused(): pl.pallas_call(functools.partial(kernel, lines), out_shape=jax.ShapeDtype...  71.2 us
    unnamed x1, local copies, waits for them, and re-layouts  1.58 us

profile of v1, /device:TPU:0, one launch (start us, length us, event | category | flops | bytes accessed | tf_op | source)
XLA Modules:
  0.0 72.8 jit_solution(17418484272558323225)
XLA Ops:
  0.0 71.2 %shard_map.73 = bf16[40,1792]{1,0:T(8,128)(2,1)} custom-call(bf16[40,1792]{1,0:T(8,128)(2,1)} %tokens.1, f32[1792]{0:T(1024)} %gain.1, f32[1792]{0:T(1024)} %bias.1, bf16[448,1920]{1,0:T(8,128)(2,1)} %w_in.1, f32[1920]{0:T(1024)} %b_in.1, bf16[448,1920]{1,0:T(8,128)(2,1)} %bitcast.1, f32[1792]{0:T(1024)} %b_out.1), custom_call_target="tpu_custom_call" | custom-call | tf_op jit(solution)/shard_map/pallas_call | solution.py:379
  71.2 1.6 %copy.9 = bf16[40,1792]{1,0:T(8,128)(2,1)} copy(bf16[40,1792]{1,0:T(8,128)(2,1)} %shard_map.73) | data formatting | bytes 286720
